TPU v7x, 32 devices: a whole 2x2x4 slice. The times are simulated.
32 devices in a mesh: gx: 4 (over y, core), gy: 8 (over z, x).
Axes of the slice: x: 2, y: 2, z: 4, core: 2. Of those that a mesh axis runs over, the one named last changes fastest.
Arguments:
- old_master: float32 [32, 128, 1536], P('gx', 'gy'), may hold values from -3 to 3
- old_first: float32 [32, 128, 1536], P('gx', 'gy'), may hold values from -3 to 3
- old_second: float32 [32, 128, 1536], P('gx', 'gy'), may hold values from 0.01 to 1
- new_grad: bfloat16 [32, 128, 1536], P(('gx', 'gy')), may hold values from -3072 to 3072
- counts: int32 [32, 32], P(None, ('gx', 'gy')), may hold values from 1 to 72, as said below
- old_owner: int32 [32], replicated, may hold values from 0 to 31, each once
- new_owner: int32 [32], replicated, may hold values from 0 to 31, each once
Outputs:
- new_master: float32 [32, 128, 1536], P(('gx', 'gy'))
- new_first: float32 [32, 128, 1536], P(('gx', 'gy'))
- new_second: float32 [32, 128, 1536], P(('gx', 'gy'))
Inputs may be any that keep to these rules, and one draw needn't show every extreme that they name: `old_owner`: every number of 0 to 31 appears once. `new_owner`: every number of 0 to 31 appears once. `counts`: every device routed at least one token to every expert.
All inputs are finite; a program needn't handle non-finite values.
Results may differ from a plain program's by a relative error of at most 0.0003.
Values sent between devices are 32-bit elements; how exact they have to be, the bound alone decides.
A program may use at most 64 MiB of HBM per device.

v0:
```python
import jax
import jax.numpy as jnp
from jax import lax
from jax.sharding import PartitionSpec as P

first_correction = 1.0 - 0.9**10
second_correction = 1.0 - 0.999**10


def adam_step(master, first, second, grad, slot_count):
    scaled = grad.astype(jnp.float32) / slot_count
    new_first = 0.9 * first + 0.1 * scaled
    new_second = 0.999 * second + 0.001 * scaled * scaled
    step_dir = new_first / first_correction / (jnp.sqrt(new_second / second_correction) + 1e-08)
    new_master = master - 0.01 * (step_dir + 0.1 * master)
    return (new_master, new_first, new_second)


def reorder(block, groups_x, groups_y):
    total_rows = block.shape[1]
    piece = total_rows // (groups_x * groups_y)
    shaped = block.reshape(1, groups_x, groups_y, piece, block.shape[2])
    return shaped.transpose(0, 2, 1, 3, 4).reshape(1, total_rows, block.shape[2])


def body(old_master, old_first, old_second, new_grad, counts, old_owner, new_owner):
    experts = old_owner.shape[0]
    groups_x = lax.axis_size("gx")
    groups_y = lax.axis_size("gy")
    my_slot = lax.axis_index("gx") * groups_y + lax.axis_index("gy")
    slots = jnp.arange(experts, dtype=jnp.int32)
    onehot = new_owner[:, None] == slots[None, :]
    source = jnp.sum(jnp.where(onehot, old_owner[:, None], 0), axis=0)
    local_counts = counts[:, 0].astype(jnp.float32)
    by_rows = (
        lax.all_to_all(old_master, "gx", split_axis=1, concat_axis=0, tiled=True),
        lax.all_to_all(old_first, "gx", split_axis=1, concat_axis=0, tiled=True),
        lax.all_to_all(old_second, "gx", split_axis=1, concat_axis=0, tiled=True),
    )
    permuted = tuple((jnp.take(state, source, axis=0) for state in by_rows))
    landed = lax.all_to_all(permuted, ("gx", "gy"), split_axis=0, concat_axis=1, tiled=True)
    arrived = tuple((reorder(state, groups_x, groups_y) for state in landed))
    totals = lax.psum(local_counts, ("gx", "gy"))
    slot_count = jnp.sum(jnp.where(new_owner == my_slot, totals, jnp.float32(0.0)))
    return adam_step(arrived[0], arrived[1], arrived[2], new_grad, slot_count)


def solution(mesh):
    placed = (
        P("gx", "gy", None),
        P("gx", "gy", None),
        P("gx", "gy", None),
        P(("gx", "gy"), None, None),
        P(None, ("gx", "gy")),
        P(),
        P(),
    )
    return jax.shard_map(
        body,
        mesh=mesh,
        in_specs=placed,
        out_specs=(
            P(("gx", "gy"), None, None),
            P(("gx", "gy"), None, None),
            P(("gx", "gy"), None, None),
        ),
        check_vma=False,
    )
```

profile of v0, /device:TPU:0, one launch (start us, length us, event | category | flops | bytes accessed | tf_op | source)
XLA Modules:
  0.0 156.1 jit_solution(17211418162359433335)
XLA Ops:
  0.6 2.5 %copy.67 = f32[8,16,1536]{2,0,1:T(8,128)} copy(f32[8,16,1536]{2,1,0:T(8,128)} %param.9) | data formatting | bytes 1572864 | tf_op args[0]
  3.1 4.4 %all-to-all-start = ((f32[8,16,1536]{2,0,1:T(8,128)}), f32[8,16,1536]{2,0,1:T(8,128)S(1)}, u32[]{:S(2)}, u32[]{:S(2)}) async-start(f32[8,16,1536]{2,0,1:T(8,128)} %copy.67), calls=%async_computation | async-start | bytes 1572864 | tf_op jit(solution)/shard_map/all_to_all | solution.py:36
  7.5 1.3 copy.72
  8.8 10.3 %all-to-all-done = f32[8,16,1536]{2,0,1:T(8,128)S(1)} async-done(((f32[8,16,1536]{2,0,1:T(8,128)}), f32[8,16,1536]{2,0,1:T(8,128)S(1)}, u32[]{:S(2)}, u32[]{:S(2)}) %all-to-all-start) | async-done | bytes 786464 | tf_op jit(solution)/shard_map/all_to_all | solution.py:36
  19.1 3.5 %all-to-all-start.2 = ((f32[8,16,1536]{2,0,1:T(8,128)}), f32[8,16,1536]{2,0,1:T(8,128)S(1)}, u32[]{:S(2)}, u32[]{:S(2)}) async-start(f32[8,16,1536]{2,0,1:T(8,128)} %copy.72), calls=%async_computation.2 | async-start | bytes 1572864 | tf_op jit(solution)/shard_map/all_to_all | solution.py:37
  22.6 1.3 copy.78
  24.0 10.2 %all-to-all-done.2 = f32[8,16,1536]{2,0,1:T(8,128)S(1)} async-done(((f32[8,16,1536]{2,0,1:T(8,128)}), f32[8,16,1536]{2,0,1:T(8,128)S(1)}, u32[]{:S(2)}, u32[]{:S(2)}) %all-to-all-start.2) | async-done | bytes 786464 | tf_op jit(solution)/shard_map/all_to_all | solution.py:37
  34.2 3.5 %all-to-all-start.4 = ((f32[8,16,1536]{2,0,1:T(8,128)}), f32[8,16,1536]{2,0,1:T(8,128)S(1)}, u32[]{:S(2)}, u32[]{:S(2)}) async-start(f32[8,16,1536]{2,0,1:T(8,128)} %copy.78), calls=%async_computation.4 | async-start | bytes 1572864 | tf_op jit(solution)/shard_map/all_to_all | solution.py:38
  37.9 0.5 copy.69
  38.5 1.4 copy.74
  39.9 1.0 gather_fusion
  40.9 2.2 %gather_fusion.1 = f32[32,4,1536]{2,1,0:T(4,128)S(1)} fusion(f32[32,4,1536]{2,1,0:T(4,128)} %copy.74, s32[1024]{0:T(1024)S(1)} %pad_clamp_fusion), kind=kCustom, calls=%fused_computation.1.clone | custom fusion | bytes 1572992 | tf_op jit(solution)/shard_map/jit(_take)/gather | solution.py:40
  43.1 6.2 %all-to-all-done.4 = f32[8,16,1536]{2,0,1:T(8,128)S(1)} async-done(((f32[8,16,1536]{2,0,1:T(8,128)}), f32[8,16,1536]{2,0,1:T(8,128)S(1)}, u32[]{:S(2)}, u32[]{:S(2)}) %all-to-all-start.4) | async-done | bytes 786464 | tf_op jit(solution)/shard_map/all_to_all | solution.py:38
  49.9 1.0 gather_fusion.2
  50.9 1.5 broadcast_select_fusion
  52.4 27.2 %all_to_all.81 = f32[32,4,1536]{2,1,0:T(4,128)S(1)} all-to-all(f32[32,4,1536]{2,1,0:T(4,128)S(1)} %get-tuple-element.13), channel_id=1, replica_groups=mesh['gx'=4,'gy'=8] {'gx','gy'}, dimensions={0} | all-to-all | bytes 1572864 | tf_op jit(solution)/shard_map/all_to_all | solution.py:41
  79.6 24.0 %all_to_all.82 = f32[32,4,1536]{2,1,0:T(4,128)S(1)} all-to-all(f32[32,4,1536]{2,1,0:T(4,128)S(1)} %get-tuple-element.14), channel_id=1, replica_groups=mesh['gx'=4,'gy'=8] {'gx','gy'}, dimensions={0} | all-to-all | bytes 1572864 | tf_op jit(solution)/shard_map/all_to_all | solution.py:41
  103.6 2.8 %all-to-all-start.1 = ((f32[32,4,1536]{2,1,0:T(4,128)}), f32[32,4,1536]{2,1,0:T(4,128)S(1)}, u32[]{:S(2)}, u32[]{:S(2)}) async-start(f32[32,4,1536]{2,1,0:T(4,128)} %get-tuple-element.15), calls=%async_computation.1 | async-start | bytes 1572864 | tf_op jit(solution)/shard_map/all_to_all | solution.py:41
  106.4 43.1 %psum.7 = f32[32]{0:T(128)S(1)} all-reduce(f32[32]{0:T(128)S(1)} %convert_bitcast_fusion), channel_id=1, replica_groups=mesh['gx'=4,'gy'=8] {'gx','gy'}, use_global_device_ids=true, to_apply=%region_1.3 | all-reduce | flops 32 | bytes 256 | tf_op jit(solution)/shard_map/psum | solution.py:43
  149.5 0.7 fusion.3
  150.5 0.8 copy.82
  151.6 0.8 copy.76
  152.7 0.8 copy.71
  153.7 2.5 %multiply_subtract_fusion = (f32[1,128,1536]{2,1,0:T(8,128)}, f32[1,128,1536]{2,1,0:T(8,128)}, f32[1,128,1536]{2,1,0:T(8,128)}) fusion(f32[1,128,1536]{2,0,1:T(1,128)S(1)} %bitcast.45, f32[]{:T(128)} %fusion.3, bf16[1,128,1536]{2,1,0:T(8,128)(2,1)S(1)} %copy-done.2, f32[1,128,1536]{2,0,1:T(1,128)S(1)} %bitcast.44, f32[1,128,1536]{2,0,1:T(1,128)S(1)} %bitcast.43), kind=kLoop, calls=%fused_computation.14 | loop fusion | flops 2949120 | bytes 5111812 | tf_op jit(solution)/shard_map/sub | solution.py:15
  (25 shorter events, 1.8 us)
Async XLA Ops:
  3.1 4.4 %copy-start = (f32[8,16,1536]{2,1,0:T(8,128)S(1)}, f32[8,16,1536]{2,1,0:T(8,128)}, u32[]{:S(2)}) copy-start(f32[8,16,1536]{2,1,0:T(8,128)} %param.10) | copy-start | bytes 2359300
  3.1 16.0 %all-to-all-start = ((f32[8,16,1536]{2,0,1:T(8,128)}), f32[8,16,1536]{2,0,1:T(8,128)S(1)}, u32[]{:S(2)}, u32[]{:S(2)}) async-start(f32[8,16,1536]{2,0,1:T(8,128)} %copy.67), calls=%async_computation | async-start | bytes 1572864 | tf_op jit(solution)/shard_map/all_to_all | solution.py:36
  8.8 13.8 %copy-start.1 = (f32[8,16,1536]{2,1,0:T(8,128)S(1)}, f32[8,16,1536]{2,1,0:T(8,128)}, u32[]{:S(2)}) copy-start(f32[8,16,1536]{2,1,0:T(8,128)} %param.11) | copy-start | bytes 2359300
  19.1 15.1 %all-to-all-start.2 = ((f32[8,16,1536]{2,0,1:T(8,128)}), f32[8,16,1536]{2,0,1:T(8,128)S(1)}, u32[]{:S(2)}, u32[]{:S(2)}) async-start(f32[8,16,1536]{2,0,1:T(8,128)} %copy.72), calls=%async_computation.2 | async-start | bytes 1572864 | tf_op jit(solution)/shard_map/all_to_all | solution.py:37
  24.0 13.7 %copy-start.3 = (s32[32]{0:T(128)S(1)}, s32[32]{0:T(128)}, u32[]{:S(2)}) copy-start(s32[32]{0:T(128)} %param.15) | copy-start | bytes 388
  24.0 13.8 %copy-start.4 = (s32[32]{0:T(128)S(1)}, s32[32]{0:T(128)}, u32[]{:S(2)}) copy-start(s32[32]{0:T(128)} %param.14) | copy-start | bytes 388
  34.2 15.1 %all-to-all-start.4 = ((f32[8,16,1536]{2,0,1:T(8,128)}), f32[8,16,1536]{2,0,1:T(8,128)S(1)}, u32[]{:S(2)}, u32[]{:S(2)}) async-start(f32[8,16,1536]{2,0,1:T(8,128)} %copy.78), calls=%async_computation.4 | async-start | bytes 1572864 | tf_op jit(solution)/shard_map/all_to_all | solution.py:38
  103.6 2.8 %copy-start.5 = (s32[32,1]{0,1:T(1,128)S(1)}, s32[32,1]{0,1:T(1,128)}, u32[]{:S(2)}) copy-start(s32[32,1]{0,1:T(1,128)} %param.13) | copy-start | bytes 388
  103.6 48.8 %all-to-all-start.1 = ((f32[32,4,1536]{2,1,0:T(4,128)}), f32[32,4,1536]{2,1,0:T(4,128)S(1)}, u32[]{:S(2)}, u32[]{:S(2)}) async-start(f32[32,4,1536]{2,1,0:T(4,128)} %get-tuple-element.15), calls=%async_computation.1 | async-start | bytes 1572864 | tf_op jit(solution)/shard_map/all_to_all | solution.py:41
  152.7 1.0 copy-start.2
where the time goes:
time: 157 us; the launch traced here: 156 us
  blocking collectives  94.3 us (60%)
  waiting for transfers between devices  26.7 us (17%)
  local copies, waits for them, and re-layouts  14.8 us (9%)
  starting transfers between devices  14.1 us (9%)
  other arithmetic  5.31 us (3%)
    all_to_all x2, blocking collectives, body(): lax.all_to_all(permuted, ('gx', 'gy'), split_axis=0, concat_axis=1, tiled...  51.2 us
    psum x1, blocking collectives, body(): totals = lax.psum(local_counts, ('gx', 'gy'))  43.1 us
    all_to_all x1, waiting for transfers between devices, body(): lax.all_to_all(old_master, 'gx', split_axis=1, concat_axis=0, tiled=True)  10.3 us
    all_to_all x1, waiting for transfers between devices, body(): lax.all_to_all(old_first, 'gx', split_axis=1, concat_axis=0, tiled=True)  10.2 us
    all_to_all x1, waiting for transfers between devices, body(): lax.all_to_all(old_second, 'gx', split_axis=1, concat_axis=0, tiled=True)  6.23 us
    unnamed x15, local copies, waits for them, and re-layouts  5.34 us
    all_to_all x1, starting transfers between devices, body(): lax.all_to_all(old_master, 'gx', split_axis=1, concat_axis=0, tiled=True)  4.4 us
    gather x3, local copies, waits for them, and re-layouts, body(): permuted = tuple((jnp.take(state, source, axis=0) for state in by_rows))  4.19 us
  transfers between devices with their start and end apart: 4, of which 3 were waited for; matrix products, arithmetic and copies ran while one was open for 7% of the time, Pallas kernels for 0%

commit v1 on v0

--- a/solution.py
+++ b/solution.py
@@ -24,6 +24,21 @@
 
 
 def body(old_master, old_first, old_second, new_grad, counts, old_owner, new_owner):
+
+    def make_the_loads(mat):
+        local_next = lax.psum(1, "gx")
+        seen_now = lax.axis_index("gx")
+        v_next, prior = (local_next, seen_now)
+        current_arr = mat.shape[1] // v_next
+        a_now = jnp.roll(mat, -prior * current_arr, 1)
+        log = [lax.slice_in_dim(a_now, 0, current_arr, axis=1)]
+        for m in range(1, v_next):
+            side_arr = lax.slice_in_dim(a_now, m * current_arr, (m + 1) * current_arr, axis=1)
+            opened = lax.ppermute(side_arr, "gx", [(d, (d + m) % v_next) for d in range(v_next)])
+            log.append(opened)
+        everything = jnp.concatenate(log[::-1], 0)
+        return jnp.roll(everything, (prior + 1) * log[0].shape[0], 0)
+
     experts = old_owner.shape[0]
     groups_x = lax.axis_size("gx")
     groups_y = lax.axis_size("gy")
@@ -35,7 +50,7 @@
     by_rows = (
         lax.all_to_all(old_master, "gx", split_axis=1, concat_axis=0, tiled=True),
         lax.all_to_all(old_first, "gx", split_axis=1, concat_axis=0, tiled=True),
-        lax.all_to_all(old_second, "gx", split_axis=1, concat_axis=0, tiled=True),
+        make_the_loads(old_second),
     )
     permuted = tuple((jnp.take(state, source, axis=0) for state in by_rows))
     landed = lax.all_to_all(permuted, ("gx", "gy"), split_axis=0, concat_axis=1, tiled=True)

time: 157 us -> 145 us (0.924)
  waiting for transfers between devices: 26.7 us -> 13.8 us
    all_to_all x1 -> x0, waiting for transfers between devices: 6.23 us -> none  [body(): lax.all_to_all(old_second, 'gx', split_axis=1, concat_axis=0, tiled=True)]
    all_to_all x1, waiting for transfers between devices: 10.3 us -> 4.07 us  [body(): lax.all_to_all(old_master, 'gx', split_axis=1, concat_axis=0, tiled=True)]
    all_to_all x1 -> x0, starting transfers between devices: 3.49 us -> none  [body(): lax.all_to_all(old_second, 'gx', split_axis=1, concat_axis=0, tiled=True)]
    ppermute x0 -> x3, starting transfers between devices: none -> 3.43 us  [make_the_loads(): lax.ppermute(side_arr, 'gx', [(d, (d + m) % v_next) for d in range(v_next)])]
    all_to_all x1, waiting for transfers between devices: 10.2 us -> 7.08 us  [body(): lax.all_to_all(old_first, 'gx', split_axis=1, concat_axis=0, tiled=True)]
    ppermute x0 -> x3, waiting for transfers between devices: none -> 2.7 us  [make_the_loads(): lax.ppermute(side_arr, 'gx', [(d, (d + m) % v_next) for d in range(v_next)])]
    unnamed x15 -> x21, local copies, waits for them, and re-layouts: 5.34 us -> 7.56 us
  transfers between devices with their start and end apart: 4 -> 6, of which waited for: 3 -> 3; matrix products, arithmetic and copies ran while one was open for 7% -> 10% of each run, Pallas kernels for 0% -> 0%
where the time goes in v1:
time: 145 us; the launch traced here: 144 us
  blocking collectives  93.7 us (65%)
  local copies, waits for them, and re-layouts  15.9 us (11%)
  waiting for transfers between devices  13.8 us (10%)
  starting transfers between devices  13 us (9%)
  other arithmetic  6.63 us (5%)
    all_to_all x2, blocking collectives, body(): lax.all_to_all(permuted, ('gx', 'gy'), split_axis=0, concat_axis=1, tiled...  50.6 us
    psum x1, blocking collectives, body(): totals = lax.psum(local_counts, ('gx', 'gy'))  43.1 us
    unnamed x21, local copies, waits for them, and re-layouts  7.56 us
    all_to_all x1, waiting for transfers between devices, body(): lax.all_to_all(old_first, 'gx', split_axis=1, concat_axis=0, tiled=True)  7.08 us
    all_to_all x1, waiting for transfers between devices, body(): lax.all_to_all(old_master, 'gx', split_axis=1, concat_axis=0, tiled=True)  4.07 us
    all_to_all x1, starting transfers between devices, body(): lax.all_to_all(old_first, 'gx', split_axis=1, concat_axis=0, tiled=True)  3.49 us
    all_to_all x1, starting transfers between devices, body(): lax.all_to_all(old_master, 'gx', split_axis=1, concat_axis=0, tiled=True)  3.49 us
    ppermute x3, starting transfers between devices, make_the_loads(): lax.ppermute(side_arr, 'gx', [(d, (d + m) % v_next) for d in range(v_next)])  3.43 us
  transfers between devices with their start and end apart: 6, of which 3 were waited for; matrix products, arithmetic and copies ran while one was open for 10% of the time, Pallas kernels for 0%

profile of v1, /device:TPU:0, one launch (start us, length us, event | category | flops | bytes accessed | tf_op | source)
XLA Modules:
  0.0 144.0 jit_solution(5343790603385558627)
XLA Ops:
  0.7 1.4 fusion.1
  2.2 2.6 %collective-permute-start = (f32[8,4,1536]{2,1,0:T(4,128)S(1)}, f32[8,4,1536]{2,1,0:T(4,128)S(1)}, u32[]{:S(2)}, u32[]{:S(2)}) collective-permute-start(f32[8,4,1536]{2,1,0:T(4,128)S(1)} %get-tuple-element.15), channel_id=1, source_target_pairs={{0,24},{8,0},{16,8},{24,16},{1,25},{9,1},{17,9},{25,17},{2,26},{10... | collective-permute-start | bytes 589832 | tf_op jit(solution)/shard_map/ppermute | solution.py:37
  5.6 1.3 copy.56
  7.0 3.5 %all-to-all-start = ((f32[8,16,1536]{2,0,1:T(8,128)}), f32[8,16,1536]{2,0,1:T(8,128)S(1)}, u32[]{:S(2)}, u32[]{:S(2)}) async-start(f32[8,16,1536]{2,0,1:T(8,128)} %copy.56), calls=%async_computation | async-start | bytes 1572864 | tf_op jit(solution)/shard_map/all_to_all | solution.py:51
  10.6 1.3 copy.61
  12.7 2.7 %collective-permute-done.1 = f32[8,4,1536]{2,1,0:T(4,128)S(1)} collective-permute-done((f32[8,4,1536]{2,1,0:T(4,128)S(1)}, f32[8,4,1536]{2,1,0:T(4,128)S(1)}, u32[]{:S(2)}, u32[]{:S(2)}) %collective-permute-start.1) | collective-permute-done | bytes 196640 | tf_op jit(solution)/shard_map/ppermute | solution.py:37
  16.7 0.7 slice_dynamic-update-slice_fusion
  17.4 0.7 constant_dynamic-update-slice_fusion.2
  18.8 0.7 constant_dynamic-update-slice_fusion
  19.5 4.1 %all-to-all-done = f32[8,16,1536]{2,0,1:T(8,128)S(1)} async-done(((f32[8,16,1536]{2,0,1:T(8,128)}), f32[8,16,1536]{2,0,1:T(8,128)S(1)}, u32[]{:S(2)}, u32[]{:S(2)}) %all-to-all-start) | async-done | bytes 786464 | tf_op jit(solution)/shard_map/all_to_all | solution.py:51
  23.6 3.5 %all-to-all-start.2 = ((f32[8,16,1536]{2,0,1:T(8,128)}), f32[8,16,1536]{2,0,1:T(8,128)S(1)}, u32[]{:S(2)}, u32[]{:S(2)}) async-start(f32[8,16,1536]{2,0,1:T(8,128)} %copy.61), calls=%async_computation.2 | async-start | bytes 1572864 | tf_op jit(solution)/shard_map/all_to_all | solution.py:52
  27.8 1.2 constant_dynamic-slice_fusion
  29.0 1.0 gather_fusion.2
  30.6 1.0 gather_fusion
  31.6 7.1 %all-to-all-done.2 = f32[8,16,1536]{2,0,1:T(8,128)S(1)} async-done(((f32[8,16,1536]{2,0,1:T(8,128)}), f32[8,16,1536]{2,0,1:T(8,128)S(1)}, u32[]{:S(2)}, u32[]{:S(2)}) %all-to-all-start.2) | async-done | bytes 786464 | tf_op jit(solution)/shard_map/all_to_all | solution.py:52
  39.3 1.0 gather_fusion.1
  40.3 1.5 %broadcast_select_fusion = (f32[32,4,1536]{2,1,0:T(4,128)S(1)}, f32[32,4,1536]{2,1,0:T(4,128)S(1)}, f32[32,4,1536]{2,1,0:T(4,128)}) fusion(f32[32,4,1536]{2,1,0:T(4,128)S(1)} %gather_fusion.2, pred[32]{0:T(512)(128)(4,1)S(1)} %compare_and_fusion, f32[32,4,1536]{2,1,0:T(4,128)S(1)} %gather_fusion.1, f32[32,4,1536]{2,1,0:T(4,128)S(1)} %gather_fusion), kind=kLoop, calls=%fused_computation.17 | loop fusion | flops 589824 | bytes 4718624 | tf_op jit(solution)/shard_map/jit(_take)/select_n | solution.py:55
  41.8 26.6 %all_to_all.63 = f32[32,4,1536]{2,1,0:T(4,128)S(1)} all-to-all(f32[32,4,1536]{2,1,0:T(4,128)S(1)} %get-tuple-element.16), channel_id=1, replica_groups=mesh['gx'=4,'gy'=8] {'gx','gy'}, dimensions={0} | all-to-all | bytes 1572864 | tf_op jit(solution)/shard_map/all_to_all | solution.py:56
  68.4 24.0 %all_to_all.64 = f32[32,4,1536]{2,1,0:T(4,128)S(1)} all-to-all(f32[32,4,1536]{2,1,0:T(4,128)S(1)} %get-tuple-element.17), channel_id=1, replica_groups=mesh['gx'=4,'gy'=8] {'gx','gy'}, dimensions={0} | all-to-all | bytes 1572864 | tf_op jit(solution)/shard_map/all_to_all | solution.py:56
  92.4 2.6 %all-to-all-start.1 = ((f32[32,4,1536]{2,1,0:T(4,128)}), f32[32,4,1536]{2,1,0:T(4,128)S(1)}, u32[]{:S(2)}, u32[]{:S(2)}) async-start(f32[32,4,1536]{2,1,0:T(4,128)} %get-tuple-element.18), calls=%async_computation.1 | async-start | bytes 1572864 | tf_op jit(solution)/shard_map/all_to_all | solution.py:56
  95.1 43.1 %psum.7 = f32[32]{0:T(128)S(1)} all-reduce(f32[32]{0:T(128)S(1)} %convert_bitcast_fusion), channel_id=1, replica_groups=mesh['gx'=4,'gy'=8] {'gx','gy'}, use_global_device_ids=true, to_apply=%region_1.3 | all-reduce | flops 32 | bytes 256 | tf_op jit(solution)/shard_map/psum | solution.py:58
  139.7 0.8 copy.65
  140.8 0.8 copy.60
  141.6 2.4 %multiply_subtract_fusion = (f32[1,128,1536]{2,1,0:T(8,128)}, f32[1,128,1536]{2,1,0:T(8,128)}, f32[1,128,1536]{2,1,0:T(8,128)}) fusion(f32[1,128,1536]{2,0,1:T(1,128)S(1)} %bitcast.37, f32[]{:T(128)} %fusion.3, bf16[1,128,1536]{2,1,0:T(8,128)(2,1)S(1)} %copy-done.2, f32[1,128,1536]{2,0,1:T(1,128)S(1)} %bitcast.36, f32[1,128,1536]{2,1,0:T(8,128)S(1)} %mul.97), kind=kLoop, calls=%fused_computation.15 | loop fusion | flops 2949120 | bytes 5111812 | tf_op jit(solution)/shard_map/sub | solution.py:15
  (38 shorter events, 7.4 us)
Async XLA Ops:
  0.6 5.0 %copy-start = (f32[8,16,1536]{2,1,0:T(8,128)S(1)}, f32[8,16,1536]{2,1,0:T(8,128)}, u32[]{:S(2)}) copy-start(f32[8,16,1536]{2,1,0:T(8,128)} %param.9) | copy-start | bytes 2359300
  2.2 9.8 %collective-permute-start = (f32[8,4,1536]{2,1,0:T(4,128)S(1)}, f32[8,4,1536]{2,1,0:T(4,128)S(1)}, u32[]{:S(2)}, u32[]{:S(2)}) collective-permute-start(f32[8,4,1536]{2,1,0:T(4,128)S(1)} %get-tuple-element.15), channel_id=1, source_target_pairs={{0,24},{8,0},{16,8},{24,16},{1,25},{9,1},{17,9},{25,17},{2,26},{10... | collective-permute-start | bytes 589832 | tf_op jit(solution)/shard_map/ppermute | solution.py:37
  4.8 10.5 %collective-permute-start.1 = (f32[8,4,1536]{2,1,0:T(4,128)S(1)}, f32[8,4,1536]{2,1,0:T(4,128)S(1)}, u32[]{:S(2)}, u32[]{:S(2)}) collective-permute-start(f32[8,4,1536]{2,1,0:T(4,128)S(1)} %get-tuple-element.14), channel_id=1, source_target_pairs={{0,16},{8,24},{16,0},{24,8},{1,17},{9,25},{17,1},{25,9},{2,18},{10... | collective-permute-start | bytes 589832 | tf_op jit(solution)/shard_map/ppermute | solution.py:37
  5.5 5.0 %copy-start.3 = (s32[32]{0:T(128)S(1)}, s32[32]{0:T(128)}, u32[]{:S(2)}) copy-start(s32[32]{0:T(128)} %param.15) | copy-start | bytes 388
  5.5 5.0 %copy-start.4 = (s32[32]{0:T(128)S(1)}, s32[32]{0:T(128)}, u32[]{:S(2)}) copy-start(s32[32]{0:T(128)} %param.14) | copy-start | bytes 388
  5.5 5.1 %copy-start.1 = (f32[8,16,1536]{2,1,0:T(8,128)S(1)}, f32[8,16,1536]{2,1,0:T(8,128)}, u32[]{:S(2)}) copy-start(f32[8,16,1536]{2,1,0:T(8,128)} %param.10) | copy-start | bytes 2359300
  5.5 10.6 %collective-permute-start.2 = (f32[8,4,1536]{2,1,0:T(4,128)S(1)}, f32[8,4,1536]{2,1,0:T(4,128)S(1)}, u32[]{:S(2)}, u32[]{:S(2)}) collective-permute-start(f32[8,4,1536]{2,1,0:T(4,128)S(1)} %get-tuple-element.13), channel_id=1, source_target_pairs={{0,8},{8,16},{16,24},{24,0},{1,9},{9,17},{17,25},{25,1},{2,10},{10... | collective-permute-start | bytes 589832 | tf_op jit(solution)/shard_map/ppermute | solution.py:37
  7.0 16.6 %all-to-all-start = ((f32[8,16,1536]{2,0,1:T(8,128)}), f32[8,16,1536]{2,0,1:T(8,128)S(1)}, u32[]{:S(2)}, u32[]{:S(2)}) async-start(f32[8,16,1536]{2,0,1:T(8,128)} %copy.56), calls=%async_computation | async-start | bytes 1572864 | tf_op jit(solution)/shard_map/all_to_all | solution.py:51
  23.6 15.1 %all-to-all-start.2 = ((f32[8,16,1536]{2,0,1:T(8,128)}), f32[8,16,1536]{2,0,1:T(8,128)S(1)}, u32[]{:S(2)}, u32[]{:S(2)}) async-start(f32[8,16,1536]{2,0,1:T(8,128)} %copy.61), calls=%async_computation.2 | async-start | bytes 1572864 | tf_op jit(solution)/shard_map/all_to_all | solution.py:52
  68.4 26.6 %copy-start.5 = (s32[32,1]{0,1:T(1,128)S(1)}, s32[32,1]{0,1:T(1,128)}, u32[]{:S(2)}) copy-start(s32[32,1]{0,1:T(1,128)} %param.13) | copy-start | bytes 388
  92.4 48.1 %all-to-all-start.1 = ((f32[32,4,1536]{2,1,0:T(4,128)}), f32[32,4,1536]{2,1,0:T(4,128)S(1)}, u32[]{:S(2)}, u32[]{:S(2)}) async-start(f32[32,4,1536]{2,1,0:T(4,128)} %get-tuple-element.18), calls=%async_computation.1 | async-start | bytes 1572864 | tf_op jit(solution)/shard_map/all_to_all | solution.py:56
  140.5 1.1 copy-start.2
